TPU v7x, 32 devices: a whole 2x2x4 slice. The times are simulated.
32 devices in a mesh: samp: 8 (over z, core), var: 4 (over y, x).
Axes of the slice: x: 2, y: 2, z: 4, core: 2. Of those that a mesh axis runs over, the one named last changes fastest.
Arguments:
- hap_words: int32 [2, 512, 512], P(None, 'samp', 'var'), may hold values from 0 to 1073741823
- total_counts: int32 [15360, 8192], P('samp', 'var'), may hold values from 0 to 4999
- allele_one: int32 [15360, 8192], P('samp', 'var'), may hold values from 0 to 299
- allele_two: int32 [15360, 8192], P('samp', 'var'), may hold values from 0 to 299
Outputs:
- z_total: float32 [512, 8192], P('samp', 'var')
- z_allelic: float32 [512, 8192], P('samp', 'var')
Inputs may be any that keep to these rules, and one draw needn't show every extreme that they name: Bit k, for k below 30, of hap_words[c, j, v] is haplotype c of sample 30 * j + k at variant v; higher bits are zero.
All inputs are finite; a program needn't handle non-finite values.
Results may differ from a plain program's by a relative error of at most 0.0003.
The roundings to bfloat16 on the way count: a program that leaves them out, or rounds other values in their place, can miss the bound.
Values sent between devices are 32-bit elements; how exact they have to be, the bound alone decides.
A program may use at most 192 MiB of HBM per device.

v0:
```python
import jax
import jax.numpy as jnp
from jax import lax
from jax.sharding import PartitionSpec as P

BITS = 30


def unpack(packed):
    shifts = jnp.arange(BITS, dtype=jnp.int32)
    bit_table = jnp.bitwise_and(
        jnp.right_shift(packed[:, :, None, :], shifts[None, None, :, None]), 1
    )
    return bit_table.reshape(2, packed.shape[1] * BITS, packed.shape[2])


def features(total_part, one_part, two_part):
    log_total = jnp.log1p(total_part.astype(jnp.float32))
    one_plus = one_part.astype(jnp.float32) + 1.0
    two_plus = two_part.astype(jnp.float32) + 1.0
    log_ratio = jnp.log(one_plus / two_plus)
    weight = 1.0 / (1.0 / one_plus + 1.0 / two_plus)
    return (log_total, (weight * log_ratio).astype(jnp.bfloat16), weight.astype(jnp.bfloat16))


def finish(pair_sums, dos_margin, gene_margin, sample_count):
    dos_sum, dos_sq = (dos_margin[0], dos_margin[1])
    gene_sum, gene_sq = (gene_margin[0], gene_margin[1])
    dosage_var = dos_sq - dos_sum * dos_sum / sample_count
    gene_var = gene_sq - gene_sum * gene_sum / sample_count
    covariance = pair_sums[0] - dos_sum[:, None] * gene_sum[None, :] / sample_count
    z_total = (
        jnp.sqrt(sample_count)
        * covariance
        / jnp.sqrt((dosage_var[:, None] + 1.0) * (gene_var[None, :] + 1.0))
    )
    z_allelic = pair_sums[1] / jnp.sqrt(pair_sums[2] + 1.0)
    return (z_total, z_allelic)


def per_device(hap_words, total_counts, allele_one, allele_two):
    panel_words = lax.all_gather(hap_words, "var", axis=2, tiled=True)
    bit_table = unpack(panel_words)
    dosage_b = (bit_table[0] + bit_table[1] - 1).astype(jnp.bfloat16)
    phase_int = bit_table[0] - bit_table[1]
    phase_b = phase_int.astype(jnp.bfloat16)
    phase_sq_b = (phase_int * phase_int).astype(jnp.bfloat16)
    dos_margin = jnp.stack(
        [
            jnp.sum(dosage_b, axis=0, dtype=jnp.float32),
            jnp.sum(dosage_b * dosage_b, axis=0, dtype=jnp.float32),
        ]
    )
    log_total, weighted_b, weight_b = features(total_counts, allele_one, allele_two)
    gene_margin = jnp.stack([jnp.sum(log_total, axis=0), jnp.sum(log_total * log_total, axis=0)])
    cross_total = jnp.einsum(
        "sv,sg->vg", dosage_b, log_total.astype(jnp.bfloat16), preferred_element_type=jnp.float32
    )
    cross_allelic = jnp.einsum("sv,sg->vg", phase_b, weighted_b, preferred_element_type=jnp.float32)
    het_weight = jnp.einsum("sv,sg->vg", phase_sq_b, weight_b, preferred_element_type=jnp.float32)
    pair_sums = jnp.stack([cross_total, cross_allelic, het_weight])
    sample_groups = lax.axis_size("samp")
    sample_count = jnp.float32(bit_table.shape[1] * sample_groups)
    own_pairs, own_dos = (
        lax.psum_scatter(pair_sums, "samp", scatter_dimension=1, tiled=True),
        lax.psum_scatter(dos_margin, "samp", scatter_dimension=1, tiled=True),
    )
    summed_genes = lax.psum(gene_margin, "samp")
    return finish(own_pairs, own_dos, summed_genes, sample_count)


def solution(mesh):
    in_specs = (P(None, "samp", "var"), P("samp", "var"), P("samp", "var"), P("samp", "var"))
    out_specs = (P("samp", "var"), P("samp", "var"))
    return jax.shard_map(
        per_device, mesh=mesh, in_specs=in_specs, out_specs=out_specs, check_vma=False
    )
```

profile of v0, /device:TPU:0, one launch (start us, length us, event | category | flops | bytes accessed | tf_op | source)
XLA Modules:
  0.0 234.2 jit_solution(2295800869853956210)
XLA Ops:
  7.2 0.0 reduce-scatter.7.cloned.1.call-start
  7.2 11.8 %all_gather.3 = s32[2,64,512]{2,1,0:T(8,128)S(1)} all-gather(s32[2,64,128]{2,1,0:T(8,128)} %param.4), channel_id=1, replica_groups=mesh['samp'=8,'var'=4] {'var'}, dimensions={2}, use_global_device_ids=true | all-gather | bytes 327680 | tf_op jit(solution)/shard_map/all_gather | solution.py:42
  19.0 1.3 shift-right-arithmetic_and_fusion
  20.3 0.0 copy-start
  20.3 3.2 %copy-done = s32[2,64,30,512]{3,2,1,0:T(8,128)} copy-done((s32[2,64,30,512]{3,2,1,0:T(8,128)}, s32[2,64,30,512]{3,2,1,0:T(8,128)S(1)}, u32[]{:S(2)}) %copy-start) | copy-done | bytes 7864344
  23.5 1.4 convert_reduce_fusion.1
  24.9 0.9 copy.6
  25.8 0.0 reduce-scatter.7.cloned.1.call-update
  25.8 0.2 reduce-scatter.5.cloned.1.call-start
  26.0 6.9 %fusion.14 = (bf16[1,64,30,512]{3,2,1,0:T(8,128)(2,1)}, bf16[1,64,30,512]{3,2,1,0:T(8,128)(2,1)}) fusion(s32[2,64,30,512]{3,2,1,0:T(8,128)} %copy-done), kind=kLoop, calls=%fused_computation.22 | loop fusion | flops 3932160 | bytes 11796480 | tf_op jit(solution)/shard_map/convert_element_type | solution.py:46
  32.9 1.5 convert_element_type.47
  34.4 2.6 %convert_element_type.51 = bf16[1920,512]{1,0:T(8,128)(2,1)S(1)} reshape(bf16[1,64,30,512]{3,2,1,0:T(8,128)(2,1)} %get-tuple-element.7) | data formatting | bytes 3932160 | tf_op jit(solution)/shard_map/convert_element_type | solution.py:46
  37.0 3.9 %convert_element_type.56 = bf16[1920,512]{1,0:T(8,128)(2,1)} reshape(bf16[1,64,30,512]{3,2,1,0:T(8,128)(2,1)} %get-tuple-element.8) | data formatting | bytes 3932160 | tf_op jit(solution)/shard_map/convert_element_type | solution.py:47
  40.9 0.0 copy-start.2
  40.9 14.6 %fusion.7 = f32[1,512,2048]{2,1,0:T(8,128)S(1)} fusion(bf16[1920,512]{1,0:T(8,128)(2,1)S(1)} %convert_element_type.51, s32[1920,2048]{1,0:T(8,128)} %param.6, s32[1920,2048]{1,0:T(8,128)} %param.7), kind=kOutput, calls=%fused_computation.19 | convolution fusion | flops 4069785600 | bytes 37617664 | tf_op jit(solution)/shard_map/sv,sg->vg/dot_general | solution.py:59
  55.5 0.0 copy-done.2
  55.5 0.0 copy-start.1
  55.5 15.1 %fusion.8 = f32[1,512,2048]{2,1,0:T(8,128)} fusion(bf16[1920,512]{1,0:T(8,128)(2,1)S(1)} %copy-done.2, s32[1920,2048]{1,0:T(8,128)} %param.6, s32[1920,2048]{1,0:T(8,128)} %param.7), kind=kOutput, calls=%fused_computation.20 | convolution fusion | flops 4061921280 | bytes 37617664 | tf_op jit(solution)/shard_map/sv,sg->vg/dot_general | solution.py:60
  70.7 0.0 copy-done.1
  70.7 12.8 %fusion.11 = f32[1,512,2048]{2,1,0:T(8,128)} fusion(bf16[1920,512]{1,0:T(8,128)(2,1)S(1)} %copy-done.1, s32[1920,2048]{1,0:T(8,128)} %param.5), kind=kOutput, calls=%fused_computation.21 | convolution fusion | flops 4034396160 | bytes 21889024 | tf_op jit(solution)/shard_map/sv,sg->vg/dot_general | solution.py:56
  83.5 9.9 %pad_maximum_fusion = f32[3,512,2048]{2,1,0:T(8,128)} fusion(f32[1,512,2048]{2,1,0:T(8,128)} %fusion.8, f32[1,512,2048]{2,1,0:T(8,128)S(1)} %fusion.7, f32[1,512,2048]{2,1,0:T(8,128)} %fusion.11), kind=kLoop, calls=%fused_computation.8 | loop fusion | flops 6291456 | bytes 25165824 | tf_op jit(solution)/shard_map/stack | solution.py:61
  93.4 0.0 reduce-scatter.5.cloned.1.call-update
  93.4 12.1 %fusion = (f32[2048]{0:T(1024)S(1)}, f32[2048]{0:T(1024)S(1)}) fusion(s32[1920,2048]{1,0:T(8,128)} %param.5), kind=kLoop, calls=%fused_computation.6 | loop fusion | flops 15724544 | bytes 15745024 | tf_op jit(solution)/shard_map/reduce_sum | solution.py:55
  105.5 28.7 %psum.7 = f32[2,2048]{1,0:T(2,128)S(1)} all-reduce(f32[2,2048]{1,0:T(2,128)S(1)} %pad_maximum_fusion.1), channel_id=1, replica_groups=mesh['samp'=8,'var'=4] {'samp'}, use_global_device_ids=true, to_apply=%region_6.0 | all-reduce | flops 4096 | bytes 32768 | tf_op jit(solution)/shard_map/psum | solution.py:68
  134.2 0.0 reduce-scatter.7.cloned.1.call-done
  134.2 0.9 fusion.24
  135.2 0.1 copy.8
  135.2 0.1 copy.9
  135.3 87.9 %reduce-scatter.5.cloned.1.call-done = f32[3,64,2048]{2,1,0:T(8,128)} async-done(((f32[3,512,2048]{2,1,0:T(8,128)}), f32[3,64,2048]{2,1,0:T(8,128)}) %reduce-scatter.5.cloned.1.call-update) | async-done | bytes 1572880 | tf_op jit(solution)/shard_map/reduce_scatter | solution.py:65
  223.2 2.1 fusion.17
  225.3 2.0 fusion.20
  (4 shorter events, 0.1 us)
Async XLA Ops:
  7.2 127.1 %reduce-scatter.7.cloned.1.call-start = ((), (), s32[]{:S(2)}) async-start(), calls=%async_computation.3 | async-start | bytes 294912
  20.3 3.2 %copy-start = (s32[2,64,30,512]{3,2,1,0:T(8,128)}, s32[2,64,30,512]{3,2,1,0:T(8,128)S(1)}, u32[]{:S(2)}) copy-start(s32[2,64,30,512]{3,2,1,0:T(8,128)S(1)} %shift-right-arithmetic_and_fusion) | copy-start | bytes 23592964
  25.8 197.5 %reduce-scatter.5.cloned.1.call-start = ((), (), s32[]{:S(2)}) async-start(), calls=%async_computation.2 | async-start | bytes 14155776 | tf_op jit(solution)/shard_map/reduce_scatter | solution.py:65
  40.9 14.6 %copy-start.2 = (bf16[1920,512]{1,0:T(8,128)(2,1)S(1)}, bf16[1920,512]{1,0:T(8,128)(2,1)}, u32[]{:S(2)}) copy-start(bf16[1920,512]{1,0:T(8,128)(2,1)} %convert_element_type.56) | copy-start | bytes 5898244
  55.5 15.2 %copy-start.1 = (bf16[1920,512]{1,0:T(8,128)(2,1)S(1)}, bf16[1920,512]{1,0:T(8,128)(2,1)}, u32[]{:S(2)}) copy-start(bf16[1920,512]{1,0:T(8,128)(2,1)} %convert_element_type.47) | copy-start | bytes 5898244
Sparse Core Ops, SparseCore 0:
  25.9 30.7 reduce-scatter.6
  93.5 129.7 reduce-scatter.4
where the time goes:
time: 235 us; the launch traced here: 234 us
  waiting for transfers between devices  88 us (37%)
  matrix products  42.6 us (18%)
  blocking collectives  40.5 us (17%)
  other arithmetic  35.6 us (15%)
  between operations  14.1 us (6%)
  local copies, waits for them, and re-layouts  13.1 us (6%)
    reduce_scatter x1, waiting for transfers between devices, per_device(): lax.psum_scatter(pair_sums, 'samp', scatter_dimension=1, tiled=True)  87.9 us
    psum x1, blocking collectives, per_device(): summed_genes = lax.psum(gene_margin, 'samp')  28.7 us
    dot_general x1, matrix products, per_device(): jnp.einsum('sv,sg->vg', phase_sq_b, weight_b, preferred_element_type=jnp....  15.1 us
    dot_general x1, matrix products, per_device(): jnp.einsum('sv,sg->vg', phase_b, weighted_b, preferred_element_type=jnp.f...  14.6 us
    dot_general x1, matrix products, per_device(): jnp.einsum('sv,sg->vg', dosage_b, log_total.astype(jnp.bfloat16), preferr...  12.8 us
    reduce_sum x1, other arithmetic, per_device(): jnp.sum(log_total, axis=0)  12.1 us
    all_gather x1, blocking collectives, per_device(): panel_words = lax.all_gather(hap_words, 'var', axis=2, tiled=True)  11.8 us
    another operation x1, other arithmetic, per_device(): pair_sums = jnp.stack([cross_total, cross_allelic, het_weight])  9.86 us
  transfers between devices with their start and end apart: 2, of which 1 were waited for; matrix products, arithmetic and copies ran while one was open for 34% of the time, Pallas kernels for 0%

commit v1 on v0

--- a/solution.py
+++ b/solution.py
@@ -38,35 +38,105 @@
     return (z_total, z_allelic)
 
 
-def per_device(hap_words, total_counts, allele_one, allele_two):
-    panel_words = lax.all_gather(hap_words, "var", axis=2, tiled=True)
-    bit_table = unpack(panel_words)
-    dosage_b = (bit_table[0] + bit_table[1] - 1).astype(jnp.bfloat16)
-    phase_int = bit_table[0] - bit_table[1]
-    phase_b = phase_int.astype(jnp.bfloat16)
-    phase_sq_b = (phase_int * phase_int).astype(jnp.bfloat16)
-    dos_margin = jnp.stack(
+def gather_words(hap_words):
+    size = lax.axis_size("var")
+    here = lax.axis_index("var")
+    blocks = [hap_words]
+    for shift in range(1, size):
+        blocks.append(
+            lax.ppermute(hap_words, "var", [((i + shift) % size, i) for i in range(size)])
+        )
+    placed = []
+    for owner in range(size):
+        steps = lax.rem(owner - here + size, size)
+        block = blocks[0]
+        for shift in range(1, size):
+            block = jnp.where(steps == shift, blocks[shift], block)
+        placed.append(block)
+    return jnp.concatenate(placed, axis=2)
+
+
+def dosage_table(packed):
+    bits = unpack(packed)
+    dosage_b = (bits[0] + bits[1] - 1).astype(jnp.bfloat16)
+    margin = jnp.stack(
         [
             jnp.sum(dosage_b, axis=0, dtype=jnp.float32),
             jnp.sum(dosage_b * dosage_b, axis=0, dtype=jnp.float32),
         ]
     )
-    log_total, weighted_b, weight_b = features(total_counts, allele_one, allele_two)
+    return (dosage_b, margin)
+
+
+def phase_tables(packed):
+    bits = unpack(packed)
+    phase = bits[0] - bits[1]
+    return (phase.astype(jnp.bfloat16), (phase * phase).astype(jnp.bfloat16))
+
+
+def pair_sum(table, feature):
+    return jnp.einsum("sv,sg->vg", table, feature, preferred_element_type=jnp.float32)
+
+
+def per_device(hap_words, total_counts, allele_one, allele_two):
+    groups = lax.axis_size("samp")
+    me = lax.axis_index("samp")
+    core = lax.rem(me, 2)
+    swap = [(i, i ^ 1) for i in range(groups)]
+    halves = [list(range(c, groups, 2)) for c in (0, 1)]
+
+    def scattered(chip_sum):
+        return lax.psum_scatter(
+            chip_sum, "samp", scatter_dimension=0, axis_index_groups=halves, tiled=True
+        )
+
+    def chip_sums(sent_table, kept_table, feature):
+        partner = lax.ppermute(pair_sum(sent_table, feature), "samp", swap)
+        return partner + lax.optimization_barrier(pair_sum(kept_table, feature))
+
+    words = gather_words(hap_words)
+    log_total = jnp.log1p(total_counts.astype(jnp.float32))
     gene_margin = jnp.stack([jnp.sum(log_total, axis=0), jnp.sum(log_total * log_total, axis=0)])
-    cross_total = jnp.einsum(
-        "sv,sg->vg", dosage_b, log_total.astype(jnp.bfloat16), preferred_element_type=jnp.float32
+    total_b = log_total.astype(jnp.bfloat16)
+    total_b, gene_margin = lax.optimization_barrier((total_b, gene_margin))
+
+    width = words.shape[2] // groups
+    split = words.reshape(2, words.shape[1], groups // 2, 2, width)
+    flat = (2, words.shape[1], groups // 2 * width)
+    low, high = (split[:, :, :, 0].reshape(flat), split[:, :, :, 1].reshape(flat))
+    sent_words = jnp.where(core == 0, high, low)
+    kept_words = jnp.where(core == 0, low, high)
+    sent_dos, sent_margin = dosage_table(sent_words)
+    kept_dos, kept_margin = dosage_table(kept_words)
+
+    sent_total = pair_sum(sent_dos, total_b)
+    kept_total = lax.optimization_barrier(pair_sum(kept_dos, total_b))
+    chip_total = lax.ppermute(sent_total, "samp", swap) + kept_total
+    chip_total, allele_one, allele_two, sent_words, kept_words = lax.optimization_barrier(
+        (chip_total, allele_one, allele_two, sent_words, kept_words)
     )
-    cross_allelic = jnp.einsum("sv,sg->vg", phase_b, weighted_b, preferred_element_type=jnp.float32)
-    het_weight = jnp.einsum("sv,sg->vg", phase_sq_b, weight_b, preferred_element_type=jnp.float32)
-    pair_sums = jnp.stack([cross_total, cross_allelic, het_weight])
-    sample_groups = lax.axis_size("samp")
-    sample_count = jnp.float32(bit_table.shape[1] * sample_groups)
-    own_pairs, own_dos = (
-        lax.psum_scatter(pair_sums, "samp", scatter_dimension=1, tiled=True),
-        lax.psum_scatter(dos_margin, "samp", scatter_dimension=1, tiled=True),
+    own_total = scattered(chip_total)
+    sent_phase, sent_sq = phase_tables(sent_words)
+    kept_phase, kept_sq = phase_tables(kept_words)
+
+    _, weighted_b, weight_b = features(total_counts, allele_one, allele_two)
+    weighted_b, weight_b = lax.optimization_barrier((weighted_b, weight_b))
+    own_allelic = scattered(chip_sums(sent_phase, kept_phase, weighted_b))
+    own_het = scattered(chip_sums(sent_sq, kept_sq, weight_b))
+
+    parts = (2, groups // 2, width)
+    even = jnp.where(core == 0, kept_margin, sent_margin).reshape(parts)
+    odd = jnp.where(core == 0, sent_margin, kept_margin).reshape(parts)
+    dos_margin = jnp.stack([even, odd], axis=2).reshape(2, groups * width)
+    margins = jnp.concatenate([gene_margin, dos_margin], axis=1)
+    margins, own_total = lax.optimization_barrier((margins, own_total))
+    margins = lax.psum(margins, "samp")
+    genes = gene_margin.shape[1]
+    own_dos = lax.dynamic_slice_in_dim(margins, genes + me * width, width, axis=1)
+    sample_count = jnp.float32(hap_words.shape[1] * BITS * groups)
+    return finish(
+        (own_total, own_allelic, own_het), own_dos, margins[:, :genes], sample_count
     )
-    summed_genes = lax.psum(gene_margin, "samp")
-    return finish(own_pairs, own_dos, summed_genes, sample_count)
 
 
 def solution(mesh):

time: 235 us -> 190 us (0.81)
  waiting for transfers between devices: 88 us -> 41.5 us
  other arithmetic: 35.6 us -> 53.1 us
  local copies, waits for them, and re-layouts: 13.1 us -> 3.98 us
  blocking collectives: 40.5 us -> 31.5 us
  starting transfers between devices: 0.26 us -> 7.17 us
  matrix products: 42.6 us -> 38.3 us
    reduce_scatter x1 -> x3, waiting for transfers between devices: 87.9 us -> 41.4 us  [scattered(): lax.psum_scatter(chip_sum, 'samp', scatter_dimension=0, axis_index_groups...]
    convert_element_type x1 -> x3, other arithmetic: 6.85 us -> 20.1 us  [the longest x1 17.8 us: features(): weight.astype(jnp.bfloat16)]
    all_gather x1 -> x0, blocking collectives: 11.8 us -> none  [per_device(): panel_words = lax.all_gather(hap_words, 'var', axis=2, tiled=True)]
    add x0 -> x3, other arithmetic: none -> 9.9 us  [the longest x2 6.6 us: chip_sums(): return partner + lax.optimization_barrier(pair_sum(kept_table, feature))]
    another operation x2 -> x1, other arithmetic: 9.87 us -> 0.01 us  [per_device(): dos_margin = jnp.stack([even, odd], axis=2).reshape(2, groups * width)]
    ppermute x0 -> x6, starting transfers between devices: none -> 6.65 us  [the longest x3 5.99 us: gather_words(): lax.ppermute(hap_words, 'var', [((i + shift) % size, i) for i in range(si...]
    convert_element_type x3 -> x6, local copies, waits for them, and re-layouts: 8.01 us -> 2.68 us  [the longest x4 2.16 us: phase_tables(): return (phase.astype(jnp.bfloat16), (phase * phase).astype(jnp.bfloat16))]
    dot_general x3 -> x6, matrix products: 42.6 us -> 38.3 us  [pair_sum(): jnp.einsum('sv,sg->vg', table, feature, preferred_element_type=jnp.float32)]
  transfers between devices with their start and end apart: 2 -> 9, of which waited for: 1 -> 1; matrix products, arithmetic and copies ran while one was open for 34% -> 42% of each run, Pallas kernels for 0% -> 0%
where the time goes in v1:
time: 190 us
  other arithmetic  53.1 us (28%)
  waiting for transfers between devices  41.5 us (22%)
  matrix products  38.3 us (20%)
  blocking collectives  31.5 us (17%)
  between operations  14 us (7%)
  starting transfers between devices  7.17 us (4%)
  local copies, waits for them, and re-layouts  3.98 us (2%)
    reduce_scatter x3, waiting for transfers between devices, scattered(): lax.psum_scatter(chip_sum, 'samp', scatter_dimension=0, axis_index_groups...  41.4 us
    dot_general x6, matrix products, pair_sum(): jnp.einsum('sv,sg->vg', table, feature, preferred_element_type=jnp.float32)  38.3 us
    psum x1, blocking collectives, per_device(): margins = lax.psum(margins, 'samp')  31.5 us
    convert_element_type x1, other arithmetic, features(): weight.astype(jnp.bfloat16)  17.8 us
    reduce_sum x1, other arithmetic, per_device(): jnp.sum(log_total, axis=0)  11.9 us
    add x2, other arithmetic, chip_sums(): return partner + lax.optimization_barrier(pair_sum(kept_table, feature))  6.6 us
    ppermute x3, starting transfers between devices, gather_words(): lax.ppermute(hap_words, 'var', [((i + shift) % size, i) for i in range(si...  5.99 us
    and x3, other arithmetic, unpack(): jnp.bitwise_and(jnp.right_shift(packed[:, :, None, :], shifts[None, None,...  3.99 us
  transfers between devices with their start and end apart: 9, of which 1 were waited for; matrix products, arithmetic and copies ran while one was open for 42% of the time, Pallas kernels for 0%

profile of v1, /device:TPU:0, one launch (start us, length us, event | category | flops | bytes accessed | tf_op | source)
XLA Modules:
  0.0 189.5 jit_solution(10633935239728044843)
XLA Ops:
  7.2 0.0 copy-start.1
  7.2 0.0 reduce-scatter.4.cloned.1.call-start
  7.2 3.1 %collective-permute-start.1 = (s32[2,64,128]{2,1,0:T(8,128)}, s32[2,64,128]{2,1,0:T(8,128)S(1)}, u32[]{:S(2)}, u32[]{:S(2)}) collective-permute-start(s32[2,64,128]{2,1,0:T(8,128)} %param.4), channel_id=1, source_target_pairs={{2,0},{3,1},{0,2},{1,3},{6,4},{7,5},{4,6},{5,7},{10,8},{11,9},{8,1... | collective-permute-start | bytes 196616 | tf_op jit(solution)/shard_map/ppermute | solution.py:47
  10.3 1.5 collective-permute-start
  11.8 1.4 collective-permute-start.2
  13.2 11.9 %fusion = (f32[2048]{0:T(1024)S(1)}, f32[2048]{0:T(1024)S(1)}, bf16[1920,2048]{1,0:T(8,128)(2,1)}) fusion(s32[1920,2048]{1,0:T(8,128)} %param.5), kind=kLoop, calls=%fused_computation.6 | loop fusion | flops 19656704 | bytes 23609344 | tf_op jit(solution)/shard_map/reduce_sum | solution.py:99
  25.1 0.0 collective-permute-done.1
  25.1 0.0 collective-permute-done
  25.1 0.0 collective-permute-done.2
  25.2 0.0 copy-done.1
  25.2 0.4 reshape.203
  25.6 1.7 fusion.8
  27.3 0.2 select_n.158
  27.5 0.6 shift-right-arithmetic_and_fusion.2
  28.2 0.7 convert_reduce_fusion
  28.8 0.3 convert_element_type.82
  29.1 6.9 %fusion.16 = f32[256,2048]{1,0:T(8,128)} fusion(bf16[1920,256]{1,0:T(8,128)(2,1)S(1)} %convert_element_type.82, bf16[1920,2048]{1,0:T(8,128)(2,1)} %get-tuple-element.14), kind=kOutput, calls=%fused_computation.56 | convolution fusion | flops 2013265920 | bytes 10944512 | tf_op jit(solution)/shard_map/sv,sg->vg/dot_general | solution.py:78
  36.0 0.0 collective-permute-start.3
  36.0 0.2 select_n.156
  36.2 0.6 shift-right-arithmetic_and_fusion.3
  36.8 0.7 convert_reduce_fusion.2
  37.5 0.3 convert_element_type.83
  37.8 5.6 %fusion.17 = f32[256,2048]{1,0:T(8,128)S(1)} fusion(bf16[1920,256]{1,0:T(8,128)(2,1)S(1)} %convert_element_type.83, bf16[1920,2048]{1,0:T(8,128)(2,1)} %get-tuple-element.14), kind=kOutput, calls=%fused_computation.57 | convolution fusion | flops 2013265920 | bytes 10944512 | tf_op jit(solution)/shard_map/sv,sg->vg/dot_general | solution.py:78
  43.4 0.0 collective-permute-done.3
  43.4 3.3 %add.98 = f32[256,2048]{1,0:T(8,128)} add(f32[256,2048]{1,0:T(8,128)} %collective-permute-done.3, f32[256,2048]{1,0:T(8,128)S(1)} %fusion.17) | non-fusion elementwise | flops 524288 | bytes 6291456 | tf_op jit(solution)/shard_map/add | solution.py:114
  46.7 0.0 reduce-scatter.4.cloned.1.call-update
  46.7 0.2 reduce-scatter.8.cloned.1.call-start
  46.9 17.8 %fusion.12 = (bf16[1920,2048]{1,0:T(8,128)(2,1)}, bf16[1920,2048]{1,0:T(8,128)(2,1)}) fusion(s32[1920,2048]{1,0:T(8,128)} %param.7, s32[1920,2048]{1,0:T(8,128)} %param.6), kind=kLoop, calls=%fused_computation.54 | loop fusion | flops 47185920 | bytes 47185920 | tf_op jit(solution)/shard_map/convert_element_type | solution.py:23
  64.7 2.7 %shift-right-arithmetic_and_fusion = (s32[2,64,30,256]{3,2,1,0:T(8,128)}, s32[2,64,30,256]{3,2,1,0:T(8,128)S(1)}) fusion(s32[2,64,256]{2,1,0:T(8,128)S(1)} %select_n.156, s32[2,64,256]{2,1,0:T(8,128)S(1)} %select_n.158), kind=kLoop, calls=%fused_computation.8 | loop fusion | flops 3932160 | bytes 8126464 | tf_op jit(solution)/shard_map/and | solution.py:11
  67.4 0.7 multiply_convert_fusion.2
  68.1 0.3 convert_element_type.93
  68.3 0.0 copy-start
  68.3 7.2 %fusion.20 = f32[256,2048]{1,0:T(8,128)} fusion(bf16[1920,256]{1,0:T(8,128)(2,1)S(1)} %convert_element_type.93, bf16[1920,2048]{1,0:T(8,128)(2,1)} %get-tuple-element.23), kind=kOutput, calls=%fused_computation.60 | convolution fusion | flops 2013265920 | bytes 10944512 | tf_op jit(solution)/shard_map/sv,sg->vg/dot_general | solution.py:78
  75.5 0.7 collective-permute-start.5
  76.2 0.0 copy-done
  76.2 1.7 multiply_convert_fusion.1
  77.8 1.4 convert_element_type.95
  79.2 5.6 %fusion.21 = f32[256,2048]{1,0:T(8,128)S(1)} fusion(bf16[1920,256]{1,0:T(8,128)(2,1)S(1)} %convert_element_type.95, bf16[1920,2048]{1,0:T(8,128)(2,1)} %get-tuple-element.23), kind=kOutput, calls=%fused_computation.61 | convolution fusion | flops 2013265920 | bytes 10944512 | tf_op jit(solution)/shard_map/sv,sg->vg/dot_general | solution.py:78
  84.8 0.0 collective-permute-done.5
  84.9 3.3 %add.108 = f32[256,2048]{1,0:T(8,128)} add(f32[256,2048]{1,0:T(8,128)} %collective-permute-done.5, f32[256,2048]{1,0:T(8,128)S(1)} %fusion.21) | non-fusion elementwise | flops 524288 | bytes 6291456 | tf_op jit(solution)/shard_map/add | solution.py:95
  88.2 0.0 reduce-scatter.8.cloned.1.call-update
  88.2 0.3 reduce-scatter.6.cloned.1.call-start
  88.5 0.3 convert_element_type.85
  88.7 7.0 %fusion.18 = f32[256,2048]{1,0:T(8,128)} fusion(bf16[1920,256]{1,0:T(8,128)(2,1)S(1)} %convert_element_type.85, bf16[1920,2048]{1,0:T(8,128)(2,1)} %get-tuple-element.21), kind=kOutput, calls=%fused_computation.58 | convolution fusion | flops 2013265920 | bytes 10944512 | tf_op jit(solution)/shard_map/sv,sg->vg/dot_general | solution.py:78
  95.8 0.0 collective-permute-start.4
  95.8 0.3 convert_element_type.91
  96.0 6.0 %fusion.19 = f32[256,2048]{1,0:T(8,128)S(1)} fusion(bf16[1920,256]{1,0:T(8,128)(2,1)S(1)} %convert_element_type.91, bf16[1920,2048]{1,0:T(8,128)(2,1)} %get-tuple-element.21), kind=kOutput, calls=%fused_computation.59 | convolution fusion | flops 2013265920 | bytes 10944512 | tf_op jit(solution)/shard_map/sv,sg->vg/dot_general | solution.py:78
  102.0 0.0 collective-permute-done.4
  102.0 3.3 %add.107 = f32[256,2048]{1,0:T(8,128)} add(f32[256,2048]{1,0:T(8,128)} %collective-permute-done.4, f32[256,2048]{1,0:T(8,128)S(1)} %fusion.19) | non-fusion elementwise | flops 524288 | bytes 6291456 | tf_op jit(solution)/shard_map/add | solution.py:95
  105.3 0.0 reduce-scatter.6.cloned.1.call-update
  105.3 0.1 stack.37
  105.4 0.1 stack.36
  105.5 0.1 stack.34
  105.6 0.1 stack.33
  105.7 0.1 reshape.204
  105.8 0.0 reduce-scatter.4.cloned.1.call-done
  105.8 31.5 %psum.7 = f32[2,2560]{1,0:T(2,128)S(1)} all-reduce(f32[2,2560]{1,0:T(2,128)S(1)} %pad_maximum_fusion), channel_id=1, replica_groups=mesh['samp'=8,'var'=4] {'samp'}, use_global_device_ids=true, to_apply=%region_7.8 | all-reduce | flops 5120 | bytes 40960 | tf_op jit(solution)/shard_map/psum | solution.py:133
  137.4 0.1 constant_dynamic-slice_fusion
  137.5 2.1 %rsqrt_multiply_fusion.1 = f32[64,2048]{1,0:T(8,128)} fusion(f32[64,2048]{1,0:T(8,128)} %reduce-scatter.4.cloned.1.call-done, f32[2048]{0:T(1024)S(1)} %bitcast.27, f32[64]{0:T(128)S(1)} %fusion.11, f32[2048]{0:T(1024)S(1)} %bitcast.26, f32[64]{0:T(128)S(1)} %slice_bitcast_fusion), kind=kLoop, calls=%fused_computation.29 | loop fusion | flops 786432 | bytes 1065472 | tf_op jit(solution)/shard_map/div | solution.py:33
  139.5 0.0 reduce-scatter.8.cloned.1.call-done
  139.5 41.4 %reduce-scatter.6.cloned.1.call-done = f32[64,2048]{1,0:T(8,128)} async-done(((f32[256,2048]{1,0:T(8,128)}), f32[64,2048]{1,0:T(8,128)}) %reduce-scatter.6.cloned.1.call-update) | async-done | bytes 524304 | tf_op jit(solution)/shard_map/reduce_scatter | solution.py:89
  180.9 2.1 %rsqrt_multiply_fusion = f32[64,2048]{1,0:T(8,128)} fusion(f32[64,2048]{1,0:T(8,128)} %reduce-scatter.6.cloned.1.call-done, f32[64,2048]{1,0:T(8,128)} %reduce-scatter.8.cloned.1.call-done), kind=kLoop, calls=%fused_computation.28 | loop fusion | flops 262144 | bytes 1572864 | tf_op jit(solution)/shard_map/div | solution.py:37
  (12 shorter events, 0.2 us)
Async XLA Ops:
  7.2 18.0 %copy-start.1 = (s32[2,64,128]{2,1,0:T(8,128)S(1)}, s32[2,64,128]{2,1,0:T(8,128)}, u32[]{:S(2)}) copy-start(s32[2,64,128]{2,1,0:T(8,128)} %param.4) | copy-start | bytes 196612
  7.2 98.7 %reduce-scatter.4.cloned.1.call-start = ((), (), s32[]{:S(2)}) async-start(), calls=%async_computation.3 | async-start | bytes 2621440 | tf_op jit(solution)/shard_map/reduce_scatter | solution.py:89
  7.2 17.9 %collective-permute-start.1 = (s32[2,64,128]{2,1,0:T(8,128)}, s32[2,64,128]{2,1,0:T(8,128)S(1)}, u32[]{:S(2)}, u32[]{:S(2)}) collective-permute-start(s32[2,64,128]{2,1,0:T(8,128)} %param.4), channel_id=1, source_target_pairs={{2,0},{3,1},{0,2},{1,3},{6,4},{7,5},{4,6},{5,7},{10,8},{11,9},{8,1... | collective-permute-start | bytes 196616 | tf_op jit(solution)/shard_map/ppermute | solution.py:47
  10.3 14.9 %collective-permute-start = (s32[2,64,128]{2,1,0:T(8,128)}, s32[2,64,128]{2,1,0:T(8,128)S(1)}, u32[]{:S(2)}, u32[]{:S(2)}) collective-permute-start(s32[2,64,128]{2,1,0:T(8,128)} %param.4), channel_id=1, source_target_pairs={{3,0},{0,1},{1,2},{2,3},{7,4},{4,5},{5,6},{6,7},{11,8},{8,9},{9,10... | collective-permute-start | bytes 196616 | tf_op jit(solution)/shard_map/ppermute | solution.py:47
  11.8 13.4 %collective-permute-start.2 = (s32[2,64,128]{2,1,0:T(8,128)}, s32[2,64,128]{2,1,0:T(8,128)S(1)}, u32[]{:S(2)}, u32[]{:S(2)}) collective-permute-start(s32[2,64,128]{2,1,0:T(8,128)} %param.4), channel_id=1, source_target_pairs={{1,0},{2,1},{3,2},{0,3},{5,4},{6,5},{7,6},{4,7},{9,8},{10,9},{11,1... | collective-permute-start | bytes 196616 | tf_op jit(solution)/shard_map/ppermute | solution.py:47
  36.0 7.4 %collective-permute-start.3 = (f32[256,2048]{1,0:T(8,128)}, f32[256,2048]{1,0:T(8,128)}, u32[]{:S(2)}, u32[]{:S(2)}) collective-permute-start(f32[256,2048]{1,0:T(8,128)} %fusion.16), channel_id=1, source_target_pairs={{0,4},{4,0},{8,12},{12,8},{16,20},{20,16},{24,28},{28,24},{1,5},{5... | collective-permute-start | bytes 6291464 | tf_op jit(solution)/shard_map/ppermute | solution.py:114
  46.7 92.8 %reduce-scatter.8.cloned.1.call-start = ((), (), s32[]{:S(2)}) async-start(), calls=%async_computation.5 | async-start | bytes 2621440 | tf_op jit(solution)/shard_map/reduce_scatter | solution.py:89
  68.3 7.8 %copy-start = (s32[2,64,30,256]{3,2,1,0:T(8,128)S(1)}, s32[2,64,30,256]{3,2,1,0:T(8,128)}, u32[]{:S(2)}) copy-start(s32[2,64,30,256]{3,2,1,0:T(8,128)} %get-tuple-element.51) | copy-start | bytes 11796484
  75.5 9.3 %collective-permute-start.5 = (f32[256,2048]{1,0:T(8,128)}, f32[256,2048]{1,0:T(8,128)}, u32[]{:S(2)}, u32[]{:S(2)}) collective-permute-start(f32[256,2048]{1,0:T(8,128)} %fusion.20), channel_id=1, source_target_pairs={{0,4},{4,0},{8,12},{12,8},{16,20},{20,16},{24,28},{28,24},{1,5},{5... | collective-permute-start | bytes 6291464 | tf_op jit(solution)/shard_map/ppermute | solution.py:94
  88.2 92.8 %reduce-scatter.6.cloned.1.call-start = ((), (), s32[]{:S(2)}) async-start(), calls=%async_computation.4 | async-start | bytes 2621440 | tf_op jit(solution)/shard_map/reduce_scatter | solution.py:89
  95.8 6.3 %collective-permute-start.4 = (f32[256,2048]{1,0:T(8,128)}, f32[256,2048]{1,0:T(8,128)}, u32[]{:S(2)}, u32[]{:S(2)}) collective-permute-start(f32[256,2048]{1,0:T(8,128)} %fusion.18), channel_id=1, source_target_pairs={{0,4},{4,0},{8,12},{12,8},{16,20},{20,16},{24,28},{28,24},{1,5},{5... | collective-permute-start | bytes 6291464 | tf_op jit(solution)/shard_map/ppermute | solution.py:94
Sparse Core Ops, SparseCore 0:
  46.8 43.1 reduce-scatter.3
  92.3 43.3 reduce-scatter.7
  138.0 42.8 reduce-scatter.5
